TPU v7x, 32 devices: a whole 2x2x4 slice. The times are simulated.
32 devices in a mesh: curve: 8 (over z, x), grp: 4 (over y, core).
Axes of the slice: x: 2, y: 2, z: 4, core: 2. Of those that a mesh axis runs over, the one named last changes fastest.
Arguments:
- state: float32 [2, 512, 4, 12288], P(None, None, 'grp', 'curve'), may hold values from -6 to 6
- coef: float32 [512, 4, 12288], P(None, 'grp', 'curve'), may hold values from 0.2 to 4
- counts: int32 [4, 8], P('grp', 'curve'), may hold values from 512 to 1536, as said below
Outputs:
- smoothed: float32 [512, 4, 8192], P(None, 'grp', 'curve')
Inputs may be any that keep to these rules, and one draw needn't show every extreme that they name: `counts`: each rank's count is 1024 plus the drift at its own end minus the drift at the end of the rank before it; drifts lie in -256 to 256, are zero before the first rank and at the last rank, so the curve holds 8192 blocks; in every curve one rank holds exactly 1536 blocks.
All inputs are finite; a program needn't handle non-finite values.
Results may differ from a plain program's by a relative error of at most 0.00002.
Values sent between devices are 32-bit elements; how exact they have to be, the bound alone decides.
A program may use at most 128 MiB of HBM per device.

v0:
```python
import jax
import jax.numpy as jnp
from jax import lax
from jax.sharding import PartitionSpec as P

AVG = 1024
HALF = 256
CAP = 1536
SWEEPS = 2


def from_behind(value, axis, steps):
    count = lax.axis_size(axis)
    initial, last = (max(0, -steps), min(count, count - steps))
    return lax.ppermute(value, axis, [(source, source + steps) for source in range(initial, last)])


def extended(block, sides, width):
    for axis, dim in sides:
        count = lax.axis_size(axis)
        forward = [(i, i + 1) for i in range(count - 1)]
        backward = [(target, source) for source, target in forward]
        low = lax.ppermute(
            lax.slice_in_dim(block, block.shape[dim] - width, None, axis=dim), axis, forward
        )
        high = lax.ppermute(lax.slice_in_dim(block, 0, width, axis=dim), axis, backward)
        block = jnp.concatenate([low, block, high], axis=dim)
    return block


def smooth(field, source, coef, left_block, right_block, low_face, high_face):
    xplus = jnp.concatenate(
        [field[1:], jnp.concatenate([field[0:1, :, :, :, 1:], right_block[0:1]], axis=4)], axis=0
    )
    xminus = jnp.concatenate(
        [jnp.concatenate([left_block[7:8], field[7:8, :, :, :, :-1]], axis=4), field[:-1]], axis=0
    )
    yplus = jnp.concatenate([field[:, 1:], high_face[:, None]], axis=1)
    yminus = jnp.concatenate([low_face[:, None], field[:, :-1]], axis=1)
    zeroes = jnp.zeros_like(field[:, :, 0:1])
    zplus = jnp.concatenate([field[:, :, 1:], zeroes], axis=2)
    zminus = jnp.concatenate([zeroes, field[:, :, :-1]], axis=2)
    total = xplus + xminus + yplus + yminus + zplus + zminus
    return (source + total) / (6.0 + coef)


def local(state, coef, counts):
    held = counts[0, 0]
    rank = lax.axis_index("curve")
    every = lax.all_gather(counts, "curve", axis=1, tiled=True)
    order = jnp.arange(every.shape[1], dtype=jnp.int32)
    before = jnp.sum(jnp.where(order < rank, every[0], 0))
    drift_prev = before - rank * AVG
    drift_next = before + held - (rank + 1) * AVG
    tail_state = lax.dynamic_slice_in_dim(state, held - HALF, HALF, 3)
    tail_coef = lax.dynamic_slice_in_dim(coef, held - HALF, HALF, 2)
    from_left = from_behind((tail_state, tail_coef), "curve", 1)
    from_right = from_behind((state[:, :, :, :HALF], coef[:, :, :HALF]), "curve", -1)
    joined_state = jnp.concatenate([from_left[0], state, from_right[0]], axis=3)
    joined_coef = jnp.concatenate([from_left[1], coef, from_right[1]], axis=2)
    slot = jnp.arange(AVG, dtype=jnp.int32)
    keep_own = slot < AVG + drift_next
    first_start = HALF - drift_prev
    second_start = HALF + CAP - AVG - drift_next
    own_state = lax.dynamic_slice_in_dim(joined_state, first_start, AVG, 3)
    next_state = lax.dynamic_slice_in_dim(joined_state, second_start, AVG, 3)
    own_coef = lax.dynamic_slice_in_dim(joined_coef, first_start, AVG, 2)
    next_coef = lax.dynamic_slice_in_dim(joined_coef, second_start, AVG, 2)
    moved = jnp.where(keep_own, own_state, next_state)
    moved_coef = jnp.where(keep_own, own_coef, next_coef)
    field = moved[0].reshape(8, 8, 8, 1, AVG)
    source = moved[1].reshape(8, 8, 8, 1, AVG)
    cellcoef = moved_coef.reshape(8, 8, 8, 1, AVG)
    for sweep in range(SWEEPS):
        widened = extended(field, (("curve", 4),), 1)
        planes = jnp.stack([field[:, 0], field[:, 7]], axis=1)
        sides = extended(planes, (("grp", 3),), 1)
        low_face = sides[:, 1, :, 0:1]
        high_face = sides[:, 0, :, 2:3]
        field = smooth(
            field, source, cellcoef, widened[..., 0:1], widened[..., -1:], low_face, high_face
        )
    return field.reshape(512, 1, AVG)


def solution(mesh):
    placed = (P(None, None, "grp", "curve"), P(None, "grp", "curve"), P("grp", "curve"))
    return jax.shard_map(
        local, mesh=mesh, in_specs=placed, out_specs=P(None, "grp", "curve"), check_vma=False
    )
```

profile of v0, /device:TPU:15, one launch (start us, length us, event | category | flops | bytes accessed | tf_op | source)
XLA Modules:
  0.0 240.0 jit_solution(8155359105987020125)
XLA Ops:
  0.7 3.7 %fusion.9 = (f32[512,1,256]{2,1,0:T(1,128)}, f32[512,1,256]{2,1,0:T(1,128)}) fusion(f32[512,1,1536]{2,1,0:T(1,128)} %param.4, s32[]{:T(128)S(6)} %select_n.25), kind=kLoop, calls=%fused_computation.28 | loop fusion | bytes 2097156 | tf_op jit(solution)/shard_map/slice | solution.py:58
  4.4 2.2 collective-permute-start.7
  6.6 4.3 %collective-permute-start.6 = (f32[512,1,256]{2,1,0:T(1,128)}, f32[512,1,256]{2,1,0:T(1,128)}, u32[]{:S(2)}, u32[]{:S(2)}) collective-permute-start(f32[512,1,256]{2,1,0:T(1,128)} %get-tuple-element.12), channel_id=1, source_target_pairs={{0,4},{4,8},{8,12},{12,16},{16,20},{20,24},{24,28},{1,5},{5,9},{9,... | collective-permute-start | bytes 1572872 | tf_op jit(solution)/shard_map/ppermute | solution.py:15
  10.8 5.9 %fusion.6 = (f32[2,512,1,256]{3,2,1,0:T(1,128)}, f32[2,512,1,256]{3,2,1,0:T(1,128)}) fusion(f32[2,512,1,1536]{3,2,1,0:T(1,128)} %param.3, s32[]{:T(128)S(6)} %select_n.25), kind=kLoop, calls=%fused_computation.25 | loop fusion | bytes 4194308 | tf_op jit(solution)/shard_map/slice | solution.py:58
  16.8 1.9 collective-permute-start.1
  19.9 4.3 %collective-permute-start = (f32[2,512,1,256]{3,2,1,0:T(1,128)}, f32[2,512,1,256]{3,2,1,0:T(1,128)}, u32[]{:S(2)}, u32[]{:S(2)}) collective-permute-start(f32[2,512,1,256]{3,2,1,0:T(1,128)} %get-tuple-element.6), channel_id=1, source_target_pairs={{0,4},{4,8},{8,12},{12,16},{16,20},{20,24},{24,28},{1,5},{5,9},{9,... | collective-permute-start | bytes 3145736 | tf_op jit(solution)/shard_map/ppermute | solution.py:15
  24.2 58.0 %all-reduce.4 = s32[8]{0:T(128)S(1)} all-reduce(s32[8]{0:T(128)S(1)} %bitcast_dynamic-update-slice_fusion), channel_id=1, replica_groups=mesh['curve'=8,'grp'=4] {'curve'}, use_global_device_ids=true, to_apply=%add.4 | all-reduce | flops 8 | bytes 64 | tf_op jit(solution)/shard_map/squeeze | solution.py:52
  85.5 2.5 %constant_dynamic-update-slice_fusion.4 = f32[512,1,2048]{2,1,0:T(1,128)S(1)} fusion(f32[512,1,2048]{2,1,0:T(1,128)S(1)} %constant_dynamic-update-slice_fusion.5, f32[512,1,1536]{2,1,0:T(1,128)S(1)} %copy-done.1), kind=kLoop, calls=%fused_computation.17 | loop fusion | bytes 6291456
  89.6 9.1 %fusion = f32[512,1,1024]{2,1,0:T(1,128)S(1)} fusion(pred[1024]{0:T(1024)(128)(4,1)S(1)} %iota_compare_fusion, f32[512,1,2048]{2,1,0:T(1,128)S(1)} %constant_dynamic-update-slice_fusion.3, s32[]{:T(128)S(6)} %select_n.27, s32[]{:T(128)S(6)} %select_n.26), kind=kLoop, calls=%fused_computation.2 | loop fusion | flops 1048576 | bytes 6292488 | tf_op jit(solution)/shard_map/add | solution.py:44
  98.7 3.0 %constant_dynamic-update-slice_fusion.2 = f32[2,512,1,2048]{3,2,1,0:T(1,128)} fusion(f32[2,512,1,256]{3,2,1,0:T(1,128)} %collective-permute-done), kind=kLoop, calls=%fused_computation.15 | loop fusion | bytes 2097152
  101.7 5.5 %constant_dynamic-update-slice_fusion.1 = f32[2,512,1,2048]{3,2,1,0:T(1,128)} fusion(f32[2,512,1,2048]{3,2,1,0:T(1,128)} %constant_dynamic-update-slice_fusion.2, f32[2,512,1,1536]{3,2,1,0:T(1,128)S(1)} %bitcast.23), kind=kLoop, calls=%fused_computation.14 | loop fusion | bytes 12582912
  107.2 3.0 %constant_dynamic-update-slice_fusion = f32[2,512,1,2048]{3,2,1,0:T(1,128)} fusion(f32[2,512,1,2048]{3,2,1,0:T(1,128)} %constant_dynamic-update-slice_fusion.1, f32[2,512,1,256]{3,2,1,0:T(1,128)} %collective-permute-done.1), kind=kLoop, calls=%fused_computation.13 | loop fusion | bytes 2097152 | tf_op jit(solution)/shard_map/concatenate | solution.py:59
  110.1 23.2 %broadcast_select_fusion = f32[2,512,1,1024]{3,2,1,0:T(1,128)} fusion(pred[1024]{0:T(1024)(128)(4,1)S(1)} %iota_compare_fusion, f32[2,512,1,2048]{3,2,1,0:T(1,128)} %constant_dynamic-update-slice_fusion, s32[]{:T(128)S(6)} %select_n.27, s32[]{:T(128)S(6)} %select_n.26), kind=kLoop, calls=%fused_computation | loop fusion | flops 1048576 | bytes 12583944 | tf_op jit(solution)/shard_map/jit(_where)/select_n | solution.py:69
  133.4 4.7 %fusion.7 = (f32[1,448,1,1024]{3,2,1,0:T(1,128)S(1)}, f32[1,448,1,1024]{3,2,1,0:T(1,128)S(1)}) fusion(f32[2,512,1,1024]{3,2,1,0:T(1,128)} %broadcast_select_fusion), kind=kLoop, calls=%fused_computation.26 | loop fusion | bytes 7340032 | tf_op jit(solution)/shard_map/slice | solution.py:33
  138.1 2.9 %fusion.8 = (f32[1,512,1,1024]{3,2,1,0:T(1,128)S(1)}, f32[1,512,1,1024]{3,2,1,0:T(1,128)S(1)}) fusion(f32[2,512,1,1024]{3,2,1,0:T(1,128)S(1)} %copy-done), kind=kLoop, calls=%fused_computation.27 | loop fusion | bytes 8388608 | tf_op jit(solution)/shard_map/slice | solution.py:71
  143.1 4.8 %collective-permute-start.4 = (f32[8,2,8,1,1024]{4,3,2,1,0:T(1,128)S(1)}, f32[8,2,8,1,1024]{4,3,2,1,0:T(1,128)S(1)}, u32[]{:S(2)}, u32[]{:S(2)}) collective-permute-start(f32[8,2,8,1,1024]{4,3,2,1,0:T(1,128)S(1)} %pad_maximum_fusion), channel_id=1, source_target_pairs={{1,0},{2,1},{3,2},{5,4},{6,5},{7,6},{9,8},{10,9},{11,10},{13,12},{... | collective-permute-start | bytes 1572872 | tf_op jit(solution)/shard_map/ppermute | solution.py:26
  147.8 3.7 %fusion.18 = (f32[8,7,8,1,1024]{4,3,2,1,0:T(1,128)S(1)}, f32[8,7,8,1,1024]{4,3,2,1,0:T(1,128)S(1)}) fusion(f32[8,8,8,1,1024]{4,3,2,1,0:T(1,128)S(1)} %bitcast.14), kind=kLoop, calls=%fused_computation.37 | loop fusion | bytes 7340032 | tf_op jit(solution)/shard_map/slice | solution.py:38
  151.5 2.5 %fusion.20 = (f32[8,8,7,1,1024]{4,3,2,1,0:T(1,128)S(1)}, f32[8,8,7,1,1024]{4,3,2,1,0:T(1,128)S(1)}) fusion(f32[8,8,8,1,1024]{4,3,2,1,0:T(1,128)S(1)} %bitcast.15), kind=kLoop, calls=%fused_computation.39 | loop fusion | bytes 7340032 | tf_op jit(solution)/shard_map/slice | solution.py:41
  154.8 1.9 collective-permute-start.2
  156.7 4.3 %collective-permute-start.3 = (f32[8,8,8,1,1]{4,3,2,1,0:T(1,128)S(1)}, f32[8,8,8,1,1]{4,3,2,1,0:T(1,128)S(1)}, u32[]{:S(2)}, u32[]{:S(2)}) collective-permute-start(f32[8,8,8,1,1]{4,3,2,1,0:T(1,128)S(1)} %get-tuple-element.28), channel_id=1, source_target_pairs={{0,4},{4,8},{8,12},{12,16},{16,20},{20,24},{24,28},{1,5},{5,9},{9,... | collective-permute-start | bytes 6152 | tf_op jit(solution)/shard_map/ppermute | solution.py:23
  161.6 5.0 %collective-permute-done.2 = f32[8,8,8,1,1]{4,3,2,1,0:T(1,128)S(1)} collective-permute-done((f32[8,8,8,1,1]{4,3,2,1,0:T(1,128)S(1)}, f32[8,8,8,1,1]{4,3,2,1,0:T(1,128)S(1)}, u32[]{:S(2)}, u32[]{:S(2)}) %collective-permute-start.2) | collective-permute-done | bytes 2080 | tf_op jit(solution)/shard_map/ppermute | solution.py:26
  166.5 4.9 %collective-permute-done.3 = f32[8,8,8,1,1]{4,3,2,1,0:T(1,128)S(1)} collective-permute-done((f32[8,8,8,1,1]{4,3,2,1,0:T(1,128)S(1)}, f32[8,8,8,1,1]{4,3,2,1,0:T(1,128)S(1)}, u32[]{:S(2)}, u32[]{:S(2)}) %collective-permute-start.3) | collective-permute-done | bytes 2080 | tf_op jit(solution)/shard_map/ppermute | solution.py:23
  171.5 16.7 %add_divide_fusion.1 = f32[8,8,8,1,1024]{4,3,2,1,0:T(1,128)S(1)} fusion(f32[8,8,8,1,1024]{4,3,2,1,0:T(1,128)S(1)} %bitcast.18, f32[8,8,8,1,1024]{4,3,2,1,0:T(1,128)S(1)} %bitcast.20, f32[8,8,7,1,1024]{4,3,2,1,0:T(1,128)S(1)} %get-tuple-element.34, f32[8,8,7,1,1024]{4,3,2,1,0:T(1,128)S(1)} %get-tuple-element.33, ...), kind=kLoop, calls=%fused_computation.10 | loop fusion | flops 6815744 | bytes 18350080 | tf_op jit(solution)/shard_map/div | solution.py:44
  190.2 3.3 %collective-permute-start.10 = (f32[8,2,8,1,1024]{4,3,2,1,0:T(1,128)S(1)}, f32[8,2,8,1,1024]{4,3,2,1,0:T(1,128)S(1)}, u32[]{:S(2)}, u32[]{:S(2)}) collective-permute-start(f32[8,2,8,1,1024]{4,3,2,1,0:T(1,128)S(1)} %pad_maximum_fusion.1), channel_id=1, source_target_pairs={{1,0},{2,1},{3,2},{5,4},{6,5},{7,6},{9,8},{10,9},{11,10},{13,12},{... | collective-permute-start | bytes 1572872 | tf_op jit(solution)/shard_map/ppermute | solution.py:26
  193.5 2.5 %fusion.15 = (f32[8,8,7,1,1024]{4,3,2,1,0:T(1,128)S(1)}, f32[8,8,7,1,1024]{4,3,2,1,0:T(1,128)S(1)}) fusion(f32[8,8,8,1,1024]{4,3,2,1,0:T(1,128)S(1)} %add_divide_fusion.1), kind=kLoop, calls=%fused_computation.34 | loop fusion | bytes 7340032 | tf_op jit(solution)/shard_map/slice | solution.py:41
  196.0 5.2 %fusion.10 = (f32[7,8,8,1,1024]{4,3,2,1,0:T(1,128)S(1)}, f32[7,8,8,1,1024]{4,3,2,1,0:T(1,128)S(1)}) fusion(f32[8,8,8,1,1024]{4,3,2,1,0:T(1,128)S(1)} %add_divide_fusion.1), kind=kLoop, calls=%fused_computation.29 | loop fusion | bytes 7340032 | tf_op jit(solution)/shard_map/slice | solution.py:33
  201.3 3.6 %fusion.13 = (f32[8,7,8,1,1024]{4,3,2,1,0:T(1,128)S(1)}, f32[8,7,8,1,1024]{4,3,2,1,0:T(1,128)S(1)}) fusion(f32[8,8,8,1,1024]{4,3,2,1,0:T(1,128)S(1)} %add_divide_fusion.1), kind=kLoop, calls=%fused_computation.32 | loop fusion | bytes 7340032 | tf_op jit(solution)/shard_map/slice | solution.py:38
  205.6 1.9 collective-permute-start.8
  207.5 4.3 %collective-permute-start.9 = (f32[8,8,8,1,1]{4,3,2,1,0:T(1,128)S(1)}, f32[8,8,8,1,1]{4,3,2,1,0:T(1,128)S(1)}, u32[]{:S(2)}, u32[]{:S(2)}) collective-permute-start(f32[8,8,8,1,1]{4,3,2,1,0:T(1,128)S(1)} %get-tuple-element.18), channel_id=1, source_target_pairs={{0,4},{4,8},{8,12},{12,16},{16,20},{20,24},{24,28},{1,5},{5,9},{9,... | collective-permute-start | bytes 6152 | tf_op jit(solution)/shard_map/ppermute | solution.py:23
  212.4 5.0 %collective-permute-done.8 = f32[8,8,8,1,1]{4,3,2,1,0:T(1,128)S(1)} collective-permute-done((f32[8,8,8,1,1]{4,3,2,1,0:T(1,128)S(1)}, f32[8,8,8,1,1]{4,3,2,1,0:T(1,128)S(1)}, u32[]{:S(2)}, u32[]{:S(2)}) %collective-permute-start.8) | collective-permute-done | bytes 2080 | tf_op jit(solution)/shard_map/ppermute | solution.py:26
  217.4 4.9 %collective-permute-done.9 = f32[8,8,8,1,1]{4,3,2,1,0:T(1,128)S(1)} collective-permute-done((f32[8,8,8,1,1]{4,3,2,1,0:T(1,128)S(1)}, f32[8,8,8,1,1]{4,3,2,1,0:T(1,128)S(1)}, u32[]{:S(2)}, u32[]{:S(2)}) %collective-permute-start.9) | collective-permute-done | bytes 2080 | tf_op jit(solution)/shard_map/ppermute | solution.py:23
  222.3 17.4 %add_divide_fusion = f32[8,8,8,1,1024]{4,3,2,1,0:T(1,128)} fusion(f32[8,8,8,1,1024]{4,3,2,1,0:T(1,128)S(1)} %bitcast.19, f32[8,8,8,1,1024]{4,3,2,1,0:T(1,128)S(1)} %bitcast.21, f32[8,8,7,1,1024]{4,3,2,1,0:T(1,128)S(1)} %get-tuple-element.24, f32[8,8,7,1,1024]{4,3,2,1,0:T(1,128)S(1)} %get-tuple-element.23, f32[8,7,8,1,1024]{4,3,2,1,0:T(1,128)S(1)} %get-tuple-element.20, ...), kind=kLoop, calls=%fused_computation.9 | loop fusion | flops 6815744 | bytes 18350080 | tf_op jit(solution)/shard_map/div | solution.py:44
  (44 shorter events, 11.6 us)
Async XLA Ops:
  4.4 83.6 %collective-permute-start.7 = (f32[512,1,256]{2,1,0:T(1,128)}, f32[512,1,256]{2,1,0:T(1,128)}, u32[]{:S(2)}, u32[]{:S(2)}) collective-permute-start(f32[512,1,256]{2,1,0:T(1,128)} %get-tuple-element.11), channel_id=1, source_target_pairs={{4,0},{8,4},{12,8},{16,12},{20,16},{24,20},{28,24},{5,1},{9,5},{13... | collective-permute-start | bytes 1572872 | tf_op jit(solution)/shard_map/ppermute | solution.py:15
  6.5 12.2 %copy-start.2 = (u32[32]{0:T(128)S(1)}, u32[32]{0:T(128)}, u32[]{:S(2)}) copy-start(u32[32]{0:T(128)} %constant.43) | copy-start | bytes 388
  6.5 78.9 %copy-start.1 = (f32[512,1,1536]{2,1,0:T(1,128)S(1)}, f32[512,1,1536]{2,1,0:T(1,128)}, u32[]{:S(2)}) copy-start(f32[512,1,1536]{2,1,0:T(1,128)} %param.4) | copy-start | bytes 9437188
  6.6 77.5 %collective-permute-start.6 = (f32[512,1,256]{2,1,0:T(1,128)}, f32[512,1,256]{2,1,0:T(1,128)}, u32[]{:S(2)}, u32[]{:S(2)}) collective-permute-start(f32[512,1,256]{2,1,0:T(1,128)} %get-tuple-element.12), channel_id=1, source_target_pairs={{0,4},{4,8},{8,12},{12,16},{16,20},{20,24},{24,28},{1,5},{5,9},{9,... | collective-permute-start | bytes 1572872 | tf_op jit(solution)/shard_map/ppermute | solution.py:15
  16.8 90.4 %collective-permute-start.1 = (f32[2,512,1,256]{3,2,1,0:T(1,128)}, f32[2,512,1,256]{3,2,1,0:T(1,128)}, u32[]{:S(2)}, u32[]{:S(2)}) collective-permute-start(f32[2,512,1,256]{3,2,1,0:T(1,128)} %get-tuple-element.5), channel_id=1, source_target_pairs={{4,0},{8,4},{12,8},{16,12},{20,16},{24,20},{28,24},{5,1},{9,5},{13... | collective-permute-start | bytes 3145736 | tf_op jit(solution)/shard_map/ppermute | solution.py:15
  19.9 78.8 %collective-permute-start = (f32[2,512,1,256]{3,2,1,0:T(1,128)}, f32[2,512,1,256]{3,2,1,0:T(1,128)}, u32[]{:S(2)}, u32[]{:S(2)}) collective-permute-start(f32[2,512,1,256]{3,2,1,0:T(1,128)} %get-tuple-element.6), channel_id=1, source_target_pairs={{0,4},{4,8},{8,12},{12,16},{16,20},{20,24},{24,28},{1,5},{5,9},{9,... | collective-permute-start | bytes 3145736 | tf_op jit(solution)/shard_map/ppermute | solution.py:15
  85.5 16.2 %slice-start = ((s8[6291456]{0:T(1024)(128)(4,1)}), s8[2097152]{0:T(1024)(128)(4,1)S(1)}, s32[]{:S(2)}) async-start(s8[6291456]{0:T(1024)(128)(4,1)} %bitcast.22), calls=%async_computation | async-start | bytes 4194304
  89.6 12.1 %slice-start.1 = ((s8[6291456]{0:T(1024)(128)(4,1)}), s8[4194304]{0:T(1024)(128)(4,1)S(1)}, s32[]{:S(2)}) async-start(s8[6291456]{0:T(1024)(128)(4,1)} %bitcast.22), calls=%async_computation.1 | async-start | bytes 8388608
  133.4 4.7 %copy-start = (f32[2,512,1,1024]{3,2,1,0:T(1,128)S(1)}, f32[2,512,1,1024]{3,2,1,0:T(1,128)}, u32[]{:S(2)}) copy-start(f32[2,512,1,1024]{3,2,1,0:T(1,128)} %broadcast_select_fusion) | copy-start | bytes 12582916
  141.5 29.8 %collective-permute-start.5 = (f32[8,2,8,1,1024]{4,3,2,1,0:T(1,128)S(1)}, f32[8,2,8,1,1024]{4,3,2,1,0:T(1,128)S(1)}, u32[]{:S(2)}, u32[]{:S(2)}) collective-permute-start(f32[8,2,8,1,1024]{4,3,2,1,0:T(1,128)S(1)} %pad_maximum_fusion), channel_id=1, source_target_pairs={{0,1},{1,2},{2,3},{4,5},{5,6},{6,7},{8,9},{9,10},{10,11},{12,13},{... | collective-permute-start | bytes 1572872 | tf_op jit(solution)/shard_map/ppermute | solution.py:23
  143.1 28.4 %collective-permute-start.4 = (f32[8,2,8,1,1024]{4,3,2,1,0:T(1,128)S(1)}, f32[8,2,8,1,1024]{4,3,2,1,0:T(1,128)S(1)}, u32[]{:S(2)}, u32[]{:S(2)}) collective-permute-start(f32[8,2,8,1,1024]{4,3,2,1,0:T(1,128)S(1)} %pad_maximum_fusion), channel_id=1, source_target_pairs={{1,0},{2,1},{3,2},{5,4},{6,5},{7,6},{9,8},{10,9},{11,10},{13,12},{... | collective-permute-start | bytes 1572872 | tf_op jit(solution)/shard_map/ppermute | solution.py:26
  154.8 11.8 %collective-permute-start.2 = (f32[8,8,8,1,1]{4,3,2,1,0:T(1,128)S(1)}, f32[8,8,8,1,1]{4,3,2,1,0:T(1,128)S(1)}, u32[]{:S(2)}, u32[]{:S(2)}) collective-permute-start(f32[8,8,8,1,1]{4,3,2,1,0:T(1,128)S(1)} %get-tuple-element.27), channel_id=1, source_target_pairs={{4,0},{8,4},{12,8},{16,12},{20,16},{24,20},{28,24},{5,1},{9,5},{13... | collective-permute-start | bytes 6152 | tf_op jit(solution)/shard_map/ppermute | solution.py:26
  156.7 14.7 %collective-permute-start.3 = (f32[8,8,8,1,1]{4,3,2,1,0:T(1,128)S(1)}, f32[8,8,8,1,1]{4,3,2,1,0:T(1,128)S(1)}, u32[]{:S(2)}, u32[]{:S(2)}) collective-permute-start(f32[8,8,8,1,1]{4,3,2,1,0:T(1,128)S(1)} %get-tuple-element.28), channel_id=1, source_target_pairs={{0,4},{4,8},{8,12},{12,16},{16,20},{20,24},{24,28},{1,5},{5,9},{9,... | collective-permute-start | bytes 6152 | tf_op jit(solution)/shard_map/ppermute | solution.py:23
  188.9 33.4 %collective-permute-start.11 = (f32[8,2,8,1,1024]{4,3,2,1,0:T(1,128)S(1)}, f32[8,2,8,1,1024]{4,3,2,1,0:T(1,128)S(1)}, u32[]{:S(2)}, u32[]{:S(2)}) collective-permute-start(f32[8,2,8,1,1024]{4,3,2,1,0:T(1,128)S(1)} %pad_maximum_fusion.1), channel_id=1, source_target_pairs={{0,1},{1,2},{2,3},{4,5},{5,6},{6,7},{8,9},{9,10},{10,11},{12,13},{... | collective-permute-start | bytes 1572872 | tf_op jit(solution)/shard_map/ppermute | solution.py:23
  190.2 32.1 %collective-permute-start.10 = (f32[8,2,8,1,1024]{4,3,2,1,0:T(1,128)S(1)}, f32[8,2,8,1,1024]{4,3,2,1,0:T(1,128)S(1)}, u32[]{:S(2)}, u32[]{:S(2)}) collective-permute-start(f32[8,2,8,1,1024]{4,3,2,1,0:T(1,128)S(1)} %pad_maximum_fusion.1), channel_id=1, source_target_pairs={{1,0},{2,1},{3,2},{5,4},{6,5},{7,6},{9,8},{10,9},{11,10},{13,12},{... | collective-permute-start | bytes 1572872 | tf_op jit(solution)/shard_map/ppermute | solution.py:26
  205.6 11.8 %collective-permute-start.8 = (f32[8,8,8,1,1]{4,3,2,1,0:T(1,128)S(1)}, f32[8,8,8,1,1]{4,3,2,1,0:T(1,128)S(1)}, u32[]{:S(2)}, u32[]{:S(2)}) collective-permute-start(f32[8,8,8,1,1]{4,3,2,1,0:T(1,128)S(1)} %get-tuple-element.17), channel_id=1, source_target_pairs={{4,0},{8,4},{12,8},{16,12},{20,16},{24,20},{28,24},{5,1},{9,5},{13... | collective-permute-start | bytes 6152 | tf_op jit(solution)/shard_map/ppermute | solution.py:26
  207.5 14.7 %collective-permute-start.9 = (f32[8,8,8,1,1]{4,3,2,1,0:T(1,128)S(1)}, f32[8,8,8,1,1]{4,3,2,1,0:T(1,128)S(1)}, u32[]{:S(2)}, u32[]{:S(2)}) collective-permute-start(f32[8,8,8,1,1]{4,3,2,1,0:T(1,128)S(1)} %get-tuple-element.18), channel_id=1, source_target_pairs={{0,4},{4,8},{8,12},{12,16},{16,20},{20,24},{24,28},{1,5},{5,9},{9,... | collective-permute-start | bytes 6152 | tf_op jit(solution)/shard_map/ppermute | solution.py:23
where the time goes:
time: 245 us; the launch traced here: 240 us
  other arithmetic  68.3 us (28%)
  blocking collectives  58 us (24%)
  local copies, waits for them, and re-layouts  55.7 us (23%)
  starting transfers between devices  35.8 us (15%)
  waiting for transfers between devices  19.7 us (8%)
  between operations  2.48 us (1%)
    squeeze x1, blocking collectives, local(): before = jnp.sum(jnp.where(order < rank, every[0], 0))  58 us
    div x2, other arithmetic, smooth(): return (source + total) / (6.0 + coef)  34.2 us
    select_n x1, other arithmetic, local(): moved = jnp.where(keep_own, own_state, next_state)  23.2 us
    unnamed x17, local copies, waits for them, and re-layouts  13.5 us
    ppermute x4, starting transfers between devices, from_behind(): lax.ppermute(value, axis, [(source, source + steps) for source in range(i...  12.6 us
    ppermute x4, starting transfers between devices, extended(): lax.ppermute(lax.slice_in_dim(block, 0, width, axis=dim), axis, backward)  11.9 us
    ppermute x4, starting transfers between devices, extended(): lax.ppermute(lax.slice_in_dim(block, block.shape[dim] - width, None, axis...  11.3 us
    slice x2, local copies, waits for them, and re-layouts, smooth(): field[1:]  9.94 us
  transfers between devices with their start and end apart: 12, of which 4 were waited for; matrix products, arithmetic and copies ran while one was open for 21% of the time, Pallas kernels for 0%

commit v1 on v0

v1 whole, which is shorter than its diff:
```python
import functools

import jax
import jax.numpy as jnp
from jax import lax
from jax.experimental import pallas as pl
from jax.experimental.pallas import tpu as pltpu
from jax.sharding import PartitionSpec as P

AVG = 1024
HALF = 256
SWEEPS = 2
LANES = 128
SIDE = 8
PAD = 8
MESH = pl.DeviceIdType.MESH


def gather_counts(n, mine, every, send_sem, recv_sem):
    me = lax.axis_index("curve")
    barrier = pltpu.get_barrier_semaphore()
    for off in range(1, n):
        peer = lax.rem(me + off, n)
        pl.semaphore_signal(barrier, inc=1, device_id={"curve": peer}, device_id_type=MESH)
    pl.semaphore_wait(barrier, n - 1)
    copies = []
    for off in range(1, n):
        copies.append(
            pltpu.make_async_remote_copy(
                src_ref=mine,
                dst_ref=every.at[me],
                send_sem=send_sem.at[off],
                recv_sem=recv_sem.at[off],
                device_id={"curve": lax.rem(me + off, n)},
                device_id_type=MESH,
            )
        )
        copies[-1].start()
    every[me] = mine[...]
    for copy in copies:
        copy.wait()


def exchange(
    n, groups, cap_rows, drift, state, coef, out, raw0, raw1, raw2, mid, head, tail, from_left, from_right,
    wide, edge_out, edge_in, load_sem, send_sem, recv_sem, face_send, face_recv, out_sem,
):
    cells = SIDE * SIDE * SIDE
    own_rows = AVG // LANES
    half_rows = HALF // LANES
    rank, group = lax.axis_index("curve"), lax.axis_index("grp")
    has_left, has_right = rank > 0, rank < n - 1
    has_low, has_high = group > 0, group < groups - 1
    sides = (
        (has_left, {"curve": rank - 1}), (has_right, {"curve": rank + 1}),
        (has_low, {"grp": group - 1}), (has_high, {"grp": group + 1}),
    )
    raw = (raw0, raw1, raw2)
    loads = []
    for f, src in enumerate((state.at[0], state.at[1], coef)):
        loads.append(
            pltpu.make_async_copy(src, raw[f].at[pl.ds(PAD, cells * cap_rows)], load_sem.at[f])
        )
        loads[-1].start()
    barrier = pltpu.get_barrier_semaphore()
    for there, device in sides:
        @pl.when(there)
        def _():
            pl.semaphore_signal(barrier, inc=1, device_id=device, device_id_type=MESH)
    pl.semaphore_wait(barrier, sum(there.astype(jnp.int32) for there, _ in sides))

    drift_prev, drift_next = drift[0], drift[1]
    shift = 4 * HALF - HALF - drift_prev
    first = lax.shift_right_logical(shift, 7) - 4 * half_rows + PAD
    part = shift & (LANES - 1)
    turn = (LANES - part) & (LANES - 1)
    lane = lax.broadcasted_iota(jnp.int32, (8, LANES), 1)
    row = lax.broadcasted_iota(jnp.int32, (8, LANES), 0)
    stay = lane >= part

    def aligned(low, high):
        return pltpu.roll(jnp.where(stay, low, high), turn, 1)

    def sent(f, to_left):
        here, there, device = (
            (head, from_right, sides[0][1]) if to_left else (tail, from_left, sides[1][1])
        )
        k = f + 3 * (0 if to_left else 1)
        return pltpu.make_async_remote_copy(
            src_ref=here.at[f], dst_ref=there.at[f], send_sem=send_sem.at[k],
            recv_sem=recv_sem.at[k], device_id=device, device_id_type=MESH,
        )

    for f in range(3):
        loads[f].wait()

        @pl.loop(0, cells // 8)
        def _(g, f=f):
            base = g * (8 * cap_rows) + first
            for w in range(half_rows):
                for put, at in ((head, w), (tail, cap_rows - half_rows + w)):
                    low = raw[f][pl.ds(base + at, 8, stride=cap_rows), :]
                    high = raw[f][pl.ds(base + at + 1, 8, stride=cap_rows), :]
                    put[f, w, pl.ds(pl.multiple_of(g * 8, 8), 8), :] = aligned(low, high)

        @pl.when(has_right)
        def _():
            sent(f, False).start()

        @pl.when(has_left)
        def _():
            sent(f, True).start()

    def middle(f, x, y, z):
        base = (x * (SIDE * SIDE) + y * SIDE + z) * cap_rows + first + half_rows
        return aligned(raw[f][pl.ds(base, own_rows), :], raw[f][pl.ds(base + 1, own_rows), :])

    @pl.loop(0, SIDE)
    def _(x):
        @pl.loop(0, SIDE)
        def _(y):
            for z in range(SIDE):
                wide[0, x + 1, y + 1, z] = middle(0, x, y, z)
                mid[0, x, y, z] = middle(1, x, y, z)
                mid[1, x, y, z] = middle(2, x, y, z) + 6.0

    block = lax.broadcasted_iota(jnp.int32, (half_rows, LANES), 0) * LANES
    block = block + lax.broadcasted_iota(jnp.int32, (half_rows, LANES), 1)
    is_left = block < drift_prev
    is_right = block + (AVG - HALF) >= AVG + drift_next

    def merge(f, add, ref, lead, off):
        @pl.loop(0, SIDE)
        def _(x):
            @pl.loop(0, SIDE)
            def _(y):
                for z in range(SIDE):
                    c = x * (SIDE * SIDE) + y * SIDE + z
                    for rows, got, mask in (
                        (pl.ds(0, half_rows), from_left, is_left),
                        (pl.ds(own_rows - half_rows, half_rows), from_right, is_right),
                    ):
                        new = jnp.concatenate(
                            [got[f, w, pl.ds(c, 1), :] for w in range(half_rows)], axis=0
                        )
                        old = ref[lead, x + off, y + off, z, rows, :]
                        ref[lead, x + off, y + off, z, rows, :] = jnp.where(mask, new + add, old)

    def arrived(f):
        @pl.when(has_left)
        def _():
            sent(f, False).wait_recv()

        @pl.when(has_right)
        def _():
            sent(f, True).wait_recv()

    def faces(b):
        source = wide.at[b]
        down = pltpu.make_async_remote_copy(
            src_ref=source.at[pl.ds(1, SIDE), 1], dst_ref=source.at[pl.ds(1, SIDE), SIDE + 1],
            send_sem=face_send.at[4 * b], recv_sem=face_recv.at[4 * b],
            device_id=sides[2][1], device_id_type=MESH,
        )
        up = pltpu.make_async_remote_copy(
            src_ref=source.at[pl.ds(1, SIDE), SIDE], dst_ref=source.at[pl.ds(1, SIDE), 0],
            send_sem=face_send.at[4 * b + 1], recv_sem=face_recv.at[4 * b + 1],
            device_id=sides[3][1], device_id_type=MESH,
        )
        back = pltpu.make_async_remote_copy(
            src_ref=edge_out.at[b, 0], dst_ref=edge_in.at[b, 1],
            send_sem=face_send.at[4 * b + 2], recv_sem=face_recv.at[4 * b + 2],
            device_id=sides[0][1], device_id_type=MESH,
        )
        ahead = pltpu.make_async_remote_copy(
            src_ref=edge_out.at[b, 1], dst_ref=edge_in.at[b, 0],
            send_sem=face_send.at[4 * b + 3], recv_sem=face_recv.at[4 * b + 3],
            device_id=sides[1][1], device_id_type=MESH,
        )
        return down, up, back, ahead

    last_lane, last_spot = lane == LANES - 1, (lane == LANES - 1) & (row == own_rows - 1)
    first_lane, first_spot = lane == 0, (lane == 0) & (row == 0)

    def send_faces(b):
        down, up, back, ahead = faces(b)
        @pl.when(has_low)
        def _():
            down.start()

        @pl.when(has_high)
        def _():
            up.start()

        @pl.loop(0, SIDE)
        def _(y):
            for z in range(SIDE):
                value = pltpu.roll(wide[b, 1, y + 1, z], LANES - 1, 1)
                carry = pltpu.roll(value, own_rows - 1, 0)
                wide[b, SIDE + 1, y + 1, z] = jnp.where(last_lane, carry, value)
                edge_out[b, 0, y, pl.ds(z, 1), :] = carry[own_rows - 1 : own_rows]
                value = pltpu.roll(wide[b, SIDE, y + 1, z], 1, 1)
                carry = pltpu.roll(value, 1, 0)
                wide[b, 0, y + 1, z] = jnp.where(first_lane, carry, value)
                edge_out[b, 1, y, pl.ds(z, 1), :] = carry[0:1]

        @pl.when(has_left)
        def _():
            back.start()

        @pl.when(has_right)
        def _():
            ahead.start()

        for there, at in ((has_low, 0), (has_high, SIDE + 1)):
            @pl.when(jnp.logical_not(there))
            def _():
                @pl.loop(0, SIDE)
                def _(x):
                    wide[b, x + 1, at] = jnp.zeros((SIDE, own_rows, LANES), jnp.float32)

        for there, at in ((has_left, 0), (has_right, 1)):
            @pl.when(jnp.logical_not(there))
            def _():
                edge_in[b, at] = jnp.zeros((SIDE, SIDE, LANES), jnp.float32)

    def take_faces(b):
        down, up, back, ahead = faces(b)
        @pl.when(has_left)
        def _():
            ahead.wait_recv()

        @pl.when(has_right)
        def _():
            back.wait_recv()

        @pl.loop(0, SIDE)
        def _(y):
            for z in range(SIDE):
                got = jnp.broadcast_to(edge_in[b, 1, y, pl.ds(z, 1), :], (8, LANES))
                old = wide[b, SIDE + 1, y + 1, z]
                wide[b, SIDE + 1, y + 1, z] = jnp.where(last_spot, got, old)
                got = jnp.broadcast_to(edge_in[b, 0, y, pl.ds(z, 1), :], (8, LANES))
                old = wide[b, 0, y + 1, z]
                wide[b, 0, y + 1, z] = jnp.where(first_spot, got, old)

        @pl.when(has_low)
        def _():
            up.wait_recv()

        @pl.when(has_high)
        def _():
            down.wait_recv()

    def sweep(b, put):
        @pl.loop(0, SIDE)
        def _(x):
            @pl.loop(0, SIDE)
            def _(y):
                line = [wide[b, x + 1, y + 1, z] for z in range(SIDE)]
                for z in range(SIDE):
                    total = wide[b, x + 2, y + 1, z] + wide[b, x, y + 1, z]
                    total = total + (wide[b, x + 1, y + 2, z] + wide[b, x + 1, y, z])
                    if z + 1 < SIDE:
                        total = total + line[z + 1]
                    if z > 0:
                        total = total + line[z - 1]
                    put(x, y, z, (mid[0, x, y, z] + total) / mid[1, x, y, z])

    arrived(0)
    merge(0, 0.0, wide, 0, 1)
    send_faces(0)
    arrived(1)
    merge(1, 0.0, mid, 0, 0)
    arrived(2)
    merge(2, 6.0, mid, 1, 0)

    def to_wide(b):
        def put(x, y, z, value):
            wide[b, x + 1, y + 1, z] = value
        return put

    def to_mid(x, y, z, value):
        mid[0, x, y, z] = value

    for b in range(SWEEPS):
        take_faces(b)
        if b + 1 < SWEEPS:
            sweep(b, to_wide(b + 1))
            send_faces(b + 1)
        else:
            sweep(b, to_mid)
    done = pltpu.make_async_copy(mid.at[0], out, out_sem)
    done.start()
    for b in range(SWEEPS):
        for (there, _), copy in zip((sides[2], sides[3], sides[0], sides[1]), faces(b)):
            @pl.when(there)
            def _():
                copy.wait_send()
    for f in range(3):
        @pl.when(has_right)
        def _():
            sent(f, False).wait_send()

        @pl.when(has_left)
        def _():
            sent(f, True).wait_send()
    done.wait()


def local(state, coef, counts):
    n, groups = lax.axis_size("curve"), lax.axis_size("grp")
    rank = lax.axis_index("curve")
    cells, cap = state.shape[1], state.shape[3]
    cap_rows, own_rows, half_rows = cap // LANES, AVG // LANES, HALF // LANES
    mine = jnp.broadcast_to(counts, (8, LANES))
    every = pl.pallas_call(
        functools.partial(gather_counts, n),
        out_shape=jax.ShapeDtypeStruct((n, 8, LANES), jnp.int32),
        in_specs=[pl.BlockSpec(memory_space=pltpu.VMEM)],
        out_specs=pl.BlockSpec(memory_space=pltpu.VMEM),
        scratch_shapes=[pltpu.SemaphoreType.DMA((n,)), pltpu.SemaphoreType.DMA((n,))],
        compiler_params=pltpu.CompilerParams(collective_id=0, has_side_effects=True),
    )(mine)[:, 0, 0]
    order = jnp.arange(n, dtype=jnp.int32)
    before = jnp.sum(jnp.where(order < rank, every, 0))
    drift_prev = before - rank * AVG
    drift = jnp.stack([drift_prev, drift_prev + counts[0, 0] - AVG])
    f32 = jnp.float32
    out = pl.pallas_call(
        functools.partial(exchange, n, groups, cap_rows),
        out_shape=jax.ShapeDtypeStruct((SIDE, SIDE, SIDE, own_rows, LANES), f32),
        in_specs=[
            pl.BlockSpec(memory_space=pltpu.SMEM),
            pl.BlockSpec(memory_space=pl.ANY),
            pl.BlockSpec(memory_space=pl.ANY),
        ],
        out_specs=pl.BlockSpec(memory_space=pl.ANY),
        scratch_shapes=[
            *[pltpu.VMEM((cells * cap_rows + 2 * PAD, LANES), f32) for _ in range(3)],
            pltpu.VMEM((2, SIDE, SIDE, SIDE, own_rows, LANES), f32),
            pltpu.VMEM((3, half_rows, cells, LANES), f32),
            pltpu.VMEM((3, half_rows, cells, LANES), f32),
            pltpu.VMEM((3, half_rows, cells, LANES), f32),
            pltpu.VMEM((3, half_rows, cells, LANES), f32),
            pltpu.VMEM((SWEEPS, SIDE + 2, SIDE + 2, SIDE, own_rows, LANES), f32),
            pltpu.VMEM((SWEEPS, 2, SIDE, SIDE, LANES), f32),
            pltpu.VMEM((SWEEPS, 2, SIDE, SIDE, LANES), f32),
            pltpu.SemaphoreType.DMA((3,)),
            pltpu.SemaphoreType.DMA((6,)),
            pltpu.SemaphoreType.DMA((6,)),
            pltpu.SemaphoreType.DMA((4 * SWEEPS,)),
            pltpu.SemaphoreType.DMA((4 * SWEEPS,)),
            pltpu.SemaphoreType.DMA,
        ],
        compiler_params=pltpu.CompilerParams(
            collective_id=1, has_side_effects=True, vmem_limit_bytes=48 * 1024 * 1024
        ),
    )(drift, state.reshape(2, cells * cap_rows, LANES), coef.reshape(cells * cap_rows, LANES))
    return out.reshape(cells, 1, AVG)


def solution(mesh):
    placed = (P(None, None, "grp", "curve"), P(None, "grp", "curve"), P("grp", "curve"))
    return jax.shard_map(
        local, mesh=mesh, in_specs=placed, out_specs=P(None, "grp", "curve"), check_vma=False
    )
```

time: 245 us -> 103 us (0.42)
  the two profiles are of different devices: /device:TPU:15 before, /device:TPU:9 now
where the time goes in v1:
time: 103 us; the launch traced here: 102 us
  Pallas kernels  95 us (92%)
  local copies, waits for them, and re-layouts  4.8 us (5%)
  between operations  1.33 us (1%)
    pallas_call x1, Pallas kernels, local(): pl.pallas_call(functools.partial(exchange, n, groups, cap_rows), out_shap...  87.9 us
    pallas_call x1, Pallas kernels, local(): pl.pallas_call(functools.partial(gather_counts, n), out_shape=jax.ShapeDt...  7.15 us
    unnamed x3, local copies, waits for them, and re-layouts  3.21 us

profile of v1, /device:TPU:9, one launch (start us, length us, event | category | flops | bytes accessed | tf_op | source)
XLA Modules:
  0.0 101.9 jit_solution(2794610287803658391)
XLA Ops:
  0.7 0.6 broadcast_in_dim.12.mine
  1.2 7.2 %shard_map.37 = s32[8,8,128]{2,1,0:T(8,128)} custom-call(s32[8,128]{1,0:T(8,128)} %broadcast_in_dim.12.mine), custom_call_target="tpu_custom_call" | custom-call | tf_op jit(solution)/shard_map/pallas_call | solution.py:317
  8.4 1.0 slice_reduce_fusion
  9.4 0.6 fusion
  10.7 0.1 pad_add_fusion.drift
  10.8 0.0 copy-start
  10.8 1.9 %copy-done = f32[512,1,1536]{2,1,0:T(1,128)S(1)} copy-done((f32[512,1,1536]{2,1,0:T(1,128)S(1)}, f32[512,1,1536]{2,1,0:T(1,128)}, u32[]{:S(2)}) %copy-start) | copy-done | bytes 3145752
  12.7 87.9 %shard_map.38 = f32[8,8,8,8,128]{4,3,2,1,0:T(8,128)S(1)} custom-call(s32[2]{0:T(128)S(1)} %pad_add_fusion.drift, f32[2,6144,128]{2,1,0:T(8,128)} %bitcast.10, f32[6144,128]{1,0:T(8,128)S(1)} %bitcast.9), custom_call_target="tpu_custom_call" | custom-call | tf_op jit(solution)/shard_map/pallas_call | solution.py:330
  100.6 1.3 %copy.8 = f32[512,1,1024]{2,1,0:T(1,128)} copy(f32[512,1,1024]{2,1,0:T(1,128)S(1)} %bitcast.8) | data formatting | bytes 4194304
Async XLA Ops:
  10.8 1.9 %copy-start = (f32[512,1,1536]{2,1,0:T(1,128)S(1)}, f32[512,1,1536]{2,1,0:T(1,128)}, u32[]{:S(2)}) copy-start(f32[512,1,1536]{2,1,0:T(1,128)} %param.4) | copy-start | bytes 9437188

commit v2 on v0

v2 whole, which is shorter than its diff:
```python
import functools

import jax
import jax.numpy as jnp
from jax import lax
from jax.experimental import pallas as pl
from jax.experimental.pallas import tpu as pltpu
from jax.sharding import PartitionSpec as P

AVG = 1024
HALF = 256
LANES = 128
SIDE = 8
PAD = 8
WIDE = 16
LEAD = 4
MESH = pl.DeviceIdType.MESH


def gather_counts(n, mine, ghost_out, every, ghost_in, send_sem, recv_sem, ghost_send, ghost_recv):
    me = lax.axis_index("curve")
    barrier = pltpu.get_barrier_semaphore()
    for off in range(1, n):
        peer = lax.rem(me + off, n)
        pl.semaphore_signal(barrier, inc=1, device_id={"curve": peer}, device_id_type=MESH)
    pl.semaphore_wait(barrier, n - 1)
    has_left, has_right = me > 0, me < n - 1
    ghosts = []
    for side, device in ((0, {"curve": me - 1}), (1, {"curve": me + 1})):
        ghosts.append(
            pltpu.make_async_remote_copy(
                src_ref=ghost_out.at[side], dst_ref=ghost_in.at[1 - side],
                send_sem=ghost_send.at[side], recv_sem=ghost_recv.at[side],
                device_id=device, device_id_type=MESH,
            )
        )
    for there, copy in zip((has_left, has_right), ghosts):
        @pl.when(there)
        def _():
            copy.start()
    copies = []
    for off in range(1, n):
        copies.append(
            pltpu.make_async_remote_copy(
                src_ref=mine,
                dst_ref=every.at[me],
                send_sem=send_sem.at[off],
                recv_sem=recv_sem.at[off],
                device_id={"curve": lax.rem(me + off, n)},
                device_id_type=MESH,
            )
        )
        copies[-1].start()
    every[me] = mine[...]
    for there, at in ((has_left, 0), (has_right, 1)):
        @pl.when(jnp.logical_not(there))
        def _():
            ghost_in[at] = jnp.zeros(ghost_in.shape[1:], jnp.float32)
    for copy in copies:
        copy.wait()
    for there, back, forth in ((has_left, 1, 0), (has_right, 0, 1)):
        @pl.when(there)
        def _():
            ghosts[back].wait_recv()
            ghosts[forth].wait_send()


def exchange(
    n, groups, cap_rows, drift, ghost, state, coef, out, raw0, raw1, raw2, wide0, wide1, source,
    inverse, out0, out1, out2, out3, in0, in1, in2, in3, face0, face1, near0, near1, inv, first_fix,
    second_fix, result, edge_out, edge_in, load_sem, send_sem, recv_sem, face_send, face_recv, out_sem,
):
    cells = SIDE * SIDE * SIDE
    own_rows = AVG // LANES
    half_rows = HALF // LANES
    rank, group = lax.axis_index("curve"), lax.axis_index("grp")
    has_left, has_right = rank > 0, rank < n - 1
    has_low, has_high = group > 0, group < groups - 1
    sides = (
        (has_left, {"curve": rank - 1}), (has_right, {"curve": rank + 1}),
        (has_low, {"grp": group - 1}), (has_high, {"grp": group + 1}),
    )
    raw = (raw0, raw1, raw2)
    loads = []
    for f, src in ((0, state.at[0]), (2, coef), (1, state.at[1])):
        load = pltpu.make_async_copy(src, raw[f].at[pl.ds(PAD, cells * cap_rows)], load_sem.at[f])
        load.start()
        loads.append((f, load))
    loads = dict(loads)
    barrier = pltpu.get_barrier_semaphore()
    for there, device in sides:
        @pl.when(there)
        def _():
            pl.semaphore_signal(barrier, inc=1, device_id=device, device_id_type=MESH)
    pl.semaphore_wait(barrier, sum(there.astype(jnp.int32) for there, _ in sides))

    drift_prev, drift_next = drift[0], drift[1]
    shift = 8 * LANES - LEAD * LANES - drift_prev
    first = lax.shift_right_logical(shift, 7) - 8 + PAD
    part = shift & (LANES - 1)
    turn = (LANES - part) & (LANES - 1)
    lane = lax.broadcasted_iota(jnp.int32, (8, LANES), 1)
    row = lax.broadcasted_iota(jnp.int32, (8, LANES), 0)
    stay = lane >= part
    low_rows, high_rows = pl.ds(0, 8), pl.ds(8, 8)
    own = pl.ds(LEAD, own_rows)
    to_left, to_right = 2, LEAD + own_rows - 8
    zero = jnp.zeros((8, LANES), jnp.float32)

    def each(fn):
        @pl.loop(0, SIDE)
        def _(x):
            @pl.loop(0, SIDE)
            def _(y):
                fn(x, y)

    def aligned(f, x, y, z, half):
        base = (x * (SIDE * SIDE) + y * SIDE + z) * cap_rows + first + 8 * half
        low, high = raw[f][pl.ds(base, 8), :], raw[f][pl.ds(base + 1, 8), :]
        return pltpu.roll(jnp.where(stay, low, high), turn, 1)

    kinds = ((out0, in0), (out1, in1), (out2, in2), (out3, in3))

    def sent(kind, side):
        return pltpu.make_async_remote_copy(
            src_ref=kinds[kind][0].at[side], dst_ref=kinds[kind][1].at[1 - side],
            send_sem=send_sem.at[2 * kind + side], recv_sem=recv_sem.at[2 * kind + side],
            device_id=sides[side][1], device_id_type=MESH,
        )

    def send(kind):
        @pl.when(has_right)
        def _():
            sent(kind, 1).start()

        @pl.when(has_left)
        def _():
            sent(kind, 0).start()

    def arrived(kind):
        @pl.when(has_left)
        def _():
            sent(kind, 1).wait_recv()

        @pl.when(has_right)
        def _():
            sent(kind, 0).wait_recv()

    def pack(put, get, planes):
        @pl.loop(0, SIDE)
        def _(x):
            for p, y in enumerate(planes):
                for z in range(SIDE):
                    put[0, p, x, z] = get(x, y, z, pl.ds(to_left, half_rows))
                    put[1, p, x, z] = get(x, y, z, pl.ds(8 + to_right, half_rows))

    outer, near_outer = (0, SIDE - 1), (0, 1, SIDE - 2, SIDE - 1)
    loads[0].wait()

    def step(x, y):
        for z in range(SIDE):
            wide0[x + 1, y + 1, z, low_rows, :] = aligned(0, x, y, z, 0)
            wide0[x + 1, y + 1, z, high_rows, :] = aligned(0, x, y, z, 1)
    each(step)
    pack(out0, lambda x, y, z, rows: wide0[x + 1, y + 1, z, rows, :], outer)
    send(0)
    loads[2].wait()

    def step(x, y):
        for z in range(SIDE):
            inverse[x, y, z, low_rows, :] = 1.0 / (aligned(2, x, y, z, 0) + 6.0)
            inverse[x, y, z, high_rows, :] = 1.0 / (aligned(2, x, y, z, 1) + 6.0)
    each(step)
    pack(out1, lambda x, y, z, rows: inverse[x, y, z, rows, :], near_outer)
    send(1)
    loads[1].wait()

    def step(x, y):
        for z in range(SIDE):
            source[x, y, z, low_rows, :] = aligned(1, x, y, z, 0)
            source[x, y, z, high_rows, :] = aligned(1, x, y, z, 1)
    each(step)

    block = row * LANES + lane - LEAD * LANES
    for side, at, planes in (
        (0, drift_prev - 1, ((wide0, 1, SIDE - 1), (wide0, 1, SIDE), (source, 0, SIDE - 1), (inverse, 0, SIDE - 1))),
        (1, AVG + drift_next, ((wide0, 1, 2), (wide0, 1, 1), (source, 0, 0), (inverse, 0, 0))),
    ):
        here = (block == at, block + 8 * LANES == at)
        for p, (ref, off, x) in enumerate(planes):
            @pl.loop(0, SIDE)
            def _(y):
                for z in range(SIDE):
                    value = ghost[side * 4 * SIDE * SIDE + p * SIDE * SIDE + y * SIDE + z]
                    for half, rows in enumerate((low_rows, high_rows)):
                        old = ref[x, y + off, z, rows, :]
                        ref[x, y + off, z, rows, :] = jnp.where(here[half], value, old)

    def borders(ref):
        @pl.loop(0, SIDE)
        def _(y):
            for z in range(SIDE):
                turned = [pltpu.roll(ref[1, y + 1, z, rows, :], LANES - 1, 1) for rows in (low_rows, high_rows)]
                carry = [pltpu.roll(value, 7, 0) for value in turned]
                carry[0] = jnp.where(row == 7, carry[1], carry[0])
                for half, rows in enumerate((low_rows, high_rows)):
                    ref[SIDE + 1, y + 1, z, rows, :] = jnp.where(lane == LANES - 1, carry[half], turned[half])
                turned = [pltpu.roll(ref[SIDE, y + 1, z, rows, :], 1, 1) for rows in (low_rows, high_rows)]
                carry = [pltpu.roll(value, 1, 0) for value in turned]
                carry[1] = jnp.where(row == 0, carry[0], carry[1])
                for half, rows in enumerate((low_rows, high_rows)):
                    ref[0, y + 1, z, rows, :] = jnp.where(lane == 0, carry[half], turned[half])

        @pl.loop(0, SIDE)
        def _(x):
            for at in (0, SIDE + 1):
                ref[x + 1, at] = jnp.zeros((SIDE, WIDE, LANES), jnp.float32)

    def sweep(ref, put):
        def step(x, y):
            for rows in (low_rows, high_rows):
                line = [ref[x + 1, y + 1, z, rows, :] for z in range(SIDE)]
                for z in range(SIDE):
                    total = ref[x + 2, y + 1, z, rows, :] + ref[x, y + 1, z, rows, :]
                    total = total + (ref[x + 1, y + 2, z, rows, :] + ref[x + 1, y, z, rows, :])
                    if z + 1 < SIDE:
                        total = total + line[z + 1]
                    if z > 0:
                        total = total + line[z - 1]
                    value = (source[x, y, z, rows, :] + total) * inverse[x, y, z, rows, :]
                    put(x, y, z, rows, value)
        each(step)

    def put(x, y, z, rows, value):
        wide1[x + 1, y + 1, z, rows, :] = value
    borders(wide0)
    sweep(wide0, put)
    pack(out2, lambda x, y, z, rows: wide1[x + 1, y + 1, z, rows, :], outer)
    send(2)

    def put(x, y, z, rows, value):
        if rows is low_rows:
            result[x, y, z, pl.ds(0, 8 - LEAD), :] = value[LEAD:]
            out3[0, x, y, z] = value[to_left : to_left + half_rows]
        else:
            result[x, y, z, pl.ds(8 - LEAD, own_rows - 8 + LEAD), :] = value[:to_right]
            out3[1, x, y, z] = value[to_right : to_right + half_rows]
    borders(wide1)
    sweep(wide1, put)

    spot = lax.broadcasted_iota(jnp.int32, (half_rows, LANES), 0) * LANES
    spot = spot + lax.broadcasted_iota(jnp.int32, (half_rows, LANES), 1)
    is_left = spot < drift_prev
    is_right = spot + (AVG - HALF) >= AVG + drift_next

    def merge(kind, to, get, planes):
        got = kinds[kind][1]
        @pl.loop(0, SIDE)
        def _(x):
            for p, y in enumerate(planes):
                for z in range(SIDE):
                    mine = get(x, y, z)
                    to[p, x, z] = mine
                    to[p, x, z, pl.ds(0, half_rows), :] = jnp.where(is_left, got[0, p, x, z], mine[:half_rows])
                    to[p, x, z, pl.ds(own_rows - half_rows, half_rows), :] = jnp.where(
                        is_right, got[1, p, x, z], mine[own_rows - half_rows :]
                    )

    def faces(b):
        face, near = ((face0, near0), (face1, near1))[b]
        down = pltpu.make_async_remote_copy(
            src_ref=face.at[0], dst_ref=near.at[1], send_sem=face_send.at[2 * b],
            recv_sem=face_recv.at[2 * b], device_id=sides[2][1], device_id_type=MESH,
        )
        up = pltpu.make_async_remote_copy(
            src_ref=face.at[1], dst_ref=near.at[0], send_sem=face_send.at[2 * b + 1],
            recv_sem=face_recv.at[2 * b + 1], device_id=sides[3][1], device_id_type=MESH,
        )
        return down, up

    def send_faces(b):
        for (there, _), copy in zip(sides[2:], faces(b)):
            @pl.when(there)
            def _():
                copy.start()
        for (there, _), at in zip(sides[2:], (0, 1)):
            @pl.when(jnp.logical_not(there))
            def _():
                @pl.loop(0, SIDE)
                def _(x):
                    (near0, near1)[b][at, x] = jnp.zeros((SIDE, own_rows, LANES), jnp.float32)

    def take_faces(b):
        down, up = faces(b)
        @pl.when(has_low)
        def _():
            up.wait_recv()

        @pl.when(has_high)
        def _():
            down.wait_recv()

    arrived(0)
    merge(0, face0, lambda x, y, z: wide0[x + 1, y + 1, z, own, :], outer)
    send_faces(0)
    arrived(1)
    merge(1, inv, lambda x, y, z: inverse[x, y, z, own, :], near_outer)
    take_faces(0)

    @pl.loop(0, SIDE)
    def _(x):
        for p, at, inner in ((0, 0, 1), (1, 3, 2)):
            for z in range(SIDE):
                fix = near0[p, x, z] * inv[at, x, z]
                first_fix[p, x + 1, z] = fix
                second_fix[inner, x, z] = fix * inv[inner, x, z]

    def edges(side):
        return pltpu.make_async_remote_copy(
            src_ref=edge_out.at[side], dst_ref=edge_in.at[1 - side],
            send_sem=face_send.at[4 + side], recv_sem=face_recv.at[4 + side],
            device_id=sides[side][1], device_id_type=MESH,
        )

    for p in range(2):
        for z in range(SIDE):
            value = pltpu.roll(first_fix[p, 1, z], LANES - 1, 1)
            carry = pltpu.roll(value, own_rows - 1, 0)
            first_fix[p, SIDE + 1, z] = jnp.where(lane == LANES - 1, carry, value)
            edge_out[0, p, pl.ds(z, 1), :] = carry[own_rows - 1 : own_rows]
            value = pltpu.roll(first_fix[p, SIDE, z], 1, 1)
            carry = pltpu.roll(value, 1, 0)
            first_fix[p, 0, z] = jnp.where(lane == 0, carry, value)
            edge_out[1, p, pl.ds(z, 1), :] = carry[0:1]
    for side in range(2):
        @pl.when(sides[side][0])
        def _():
            edges(side).start()

        @pl.when(jnp.logical_not(sides[side][0]))
        def _():
            edge_in[side] = jnp.zeros((2, SIDE, LANES), jnp.float32)
    send(3)
    arrived(2)
    merge(2, face1, lambda x, y, z: wide1[x + 1, y + 1, z, own, :], outer)

    @pl.loop(0, SIDE)
    def _(x):
        for p in range(2):
            for z in range(SIDE):
                face1[p, x, z] = face1[p, x, z] + first_fix[p, x + 1, z]
    send_faces(1)
    for side in range(2):
        @pl.when(sides[side][0])
        def _():
            edges(1 - side).wait_recv()
    last_spot = (lane == LANES - 1) & (row == own_rows - 1)
    first_spot = (lane == 0) & (row == 0)
    for p in range(2):
        for z in range(SIDE):
            got = jnp.broadcast_to(edge_in[1, p, pl.ds(z, 1), :], (8, LANES))
            first_fix[p, SIDE + 1, z] = jnp.where(last_spot, got, first_fix[p, SIDE + 1, z])
            got = jnp.broadcast_to(edge_in[0, p, pl.ds(z, 1), :], (8, LANES))
            first_fix[p, 0, z] = jnp.where(first_spot, got, first_fix[p, 0, z])
    take_faces(1)

    @pl.loop(0, SIDE)
    def _(x):
        for p, at in ((0, 0), (1, 3)):
            for z in range(SIDE):
                total = near1[p, x, z] + (first_fix[p, x, z] + first_fix[p, x + 2, z])
                if z + 1 < SIDE:
                    total = total + first_fix[p, x + 1, z + 1]
                if z > 0:
                    total = total + first_fix[p, x + 1, z - 1]
                second_fix[at, x, z] = total * inv[at, x, z]

    arrived(3)
    lo, hi = pl.ds(0, half_rows), pl.ds(own_rows - half_rows, half_rows)

    def step(x, y):
        for z in range(SIDE):
            for side, rows, mask in ((0, lo, is_left), (1, hi, is_right)):
                old = result[x, y, z, rows, :]
                result[x, y, z, rows, :] = jnp.where(mask, in3[side, x, y, z], old)
    each(step)

    @pl.loop(0, SIDE)
    def _(x):
        for p, y in enumerate(near_outer):
            for z in range(SIDE):
                result[x, y, z] = result[x, y, z] + second_fix[p, x, z]
    done = pltpu.make_async_copy(result, out, out_sem)
    done.start()
    for b in range(2):
        for (there, _), copy in zip(sides[2:], faces(b)):
            @pl.when(there)
            def _():
                copy.wait_send()
    for side in range(2):
        @pl.when(sides[side][0])
        def _():
            edges(side).wait_send()
            for kind in range(4):
                sent(kind, side).wait_send()
    done.wait()


def local(state, coef, counts):
    n, groups = lax.axis_size("curve"), lax.axis_size("grp")
    rank = lax.axis_index("curve")
    cells, cap = state.shape[1], state.shape[3]
    cap_rows, own_rows, half_rows = cap // LANES, AVG // LANES, HALF // LANES
    plane = SIDE * SIDE
    held = counts[0, 0]
    f32 = jnp.float32

    def end_block(at, outer, near):
        cell = lax.dynamic_slice_in_dim(state, at, 1, 3)[:, :, 0, 0].reshape(2, SIDE, plane)
        scale = lax.dynamic_slice_in_dim(coef, at, 1, 2)[:, 0, 0].reshape(SIDE, plane)
        return jnp.stack([cell[0, outer], cell[0, near], cell[1, near], 1.0 / (6.0 + scale[near])])

    ends = jnp.stack([end_block(0, 1, 0), end_block(held - 1, SIDE - 2, SIDE - 1)])
    ends = ends.reshape(2, 4 * plane // LANES, LANES)
    mine = jnp.broadcast_to(counts, (8, LANES))
    vmem, hbm, smem = (pl.BlockSpec(memory_space=m) for m in (pltpu.VMEM, pl.ANY, pltpu.SMEM))
    every, ghost = pl.pallas_call(
        functools.partial(gather_counts, n),
        out_shape=(jax.ShapeDtypeStruct((n, 8, LANES), jnp.int32), jax.ShapeDtypeStruct(ends.shape, f32)),
        in_specs=[vmem, vmem],
        out_specs=(vmem, vmem),
        scratch_shapes=[pltpu.SemaphoreType.DMA((k,)) for k in (n, n, 2, 2)],
        compiler_params=pltpu.CompilerParams(collective_id=0, has_side_effects=True),
    )(mine, ends)
    order = jnp.arange(n, dtype=jnp.int32)
    before = jnp.sum(jnp.where(order < rank, every[:, 0, 0], 0))
    drift_prev = before - rank * AVG
    drift = jnp.stack([drift_prev, drift_prev + held - AVG])
    side = (SIDE, SIDE)
    packed = [(2, 2) + side, (2, 4) + side, (2, 2) + side, (2, SIDE) + side]
    packed = [shape + (half_rows, LANES) for shape in packed]
    own = (own_rows, LANES)
    shapes = [(cells * cap_rows + 2 * PAD, LANES)] * 3
    shapes += [(SIDE + 2, SIDE + 2, SIDE, WIDE, LANES)] * 2 + [side + (SIDE, WIDE, LANES)] * 2
    shapes += packed + packed + [(2,) + side + own] * 4
    shapes += [(4,) + side + own, (2, SIDE + 2, SIDE) + own, (4,) + side + own, side + (SIDE,) + own]
    shapes += [(2, 2, SIDE, LANES)] * 2
    out = pl.pallas_call(
        functools.partial(exchange, n, groups, cap_rows),
        out_shape=jax.ShapeDtypeStruct((SIDE, SIDE, SIDE, own_rows, LANES), f32),
        in_specs=[smem, smem, hbm, hbm],
        out_specs=hbm,
        scratch_shapes=[pltpu.VMEM(shape, f32) for shape in shapes]
        + [pltpu.SemaphoreType.DMA((k,)) for k in (3, 8, 8, 6, 6)]
        + [pltpu.SemaphoreType.DMA],
        compiler_params=pltpu.CompilerParams(
            collective_id=1, has_side_effects=True, vmem_limit_bytes=56 * 1024 * 1024
        ),
    )(
        drift, ghost.reshape(-1), state.reshape(2, cells * cap_rows, LANES),
        coef.reshape(cells * cap_rows, LANES),
    )
    return out.reshape(cells, 1, AVG)


def solution(mesh):
    placed = (P(None, None, "grp", "curve"), P(None, "grp", "curve"), P("grp", "curve"))
    return jax.shard_map(
        local, mesh=mesh, in_specs=placed, out_specs=P(None, "grp", "curve"), check_vma=False
    )
```

time: 245 us -> 87.6 us (0.36)
  the two profiles are of different devices: /device:TPU:15 before, /device:TPU:9 now
where the time goes in v2:
time: 87.6 us; the launch traced here: 87.3 us
  Pallas kernels  67.6 us (77%)
  local copies, waits for them, and re-layouts  14.6 us (17%)
  other arithmetic  3.72 us (4%)
  between operations  1.34 us (2%)
    pallas_call x1, Pallas kernels, local(): pl.pallas_call(functools.partial(exchange, n, groups, cap_rows), out_shap...  60.4 us
    dynamic_slice x1, local copies, waits for them, and re-layouts, end_block(): lax.dynamic_slice_in_dim(state, at, 1, 3)[:, :, 0, 0]  8.34 us
    pallas_call x1, Pallas kernels, local(): pl.pallas_call(functools.partial(gather_counts, n), out_shape=(jax.ShapeD...  7.22 us
    unnamed x1, local copies, waits for them, and re-layouts  4.35 us
    div x1, other arithmetic, end_block(): 1.0 / (6.0 + scale[near])  1.86 us

profile of v2, /device:TPU:9, one launch (start us, length us, event | category | flops | bytes accessed | tf_op | source)
XLA Modules:
  0.0 87.3 jit_solution(4836969347642695007)
XLA Ops:
  0.7 1.9 %fusion.1 = (f32[64]{0:T(128)S(1)}, f32[64]{0:T(128)S(1)}) fusion(f32[512,1,1536]{2,1,0:T(1,128)} %param.4, s32[]{:T(128)S(6)} %add.43, s32[]{:T(128)S(6)} %select_n.8), kind=kLoop, calls=%fused_computation.5 | loop fusion | flops 256 | bytes 1032 | tf_op jit(solution)/shard_map/div | solution.py:421
  2.5 0.6 broadcast_in_dim.12.mine
  3.1 8.3 %slice_reduce_fusion = (f32[2,512]{1,0:T(2,128)S(1)}, f32[2,512]{1,0:T(2,128)S(1)}) fusion(f32[2,512,1,1536]{3,2,1,0:T(1,128)} %param.3, s32[]{:T(128)S(6)} %select_n.8), kind=kLoop, calls=%fused_computation.1 | loop fusion | bytes 16388 | tf_op jit(solution)/shard_map/dynamic_slice | solution.py:419
  11.5 0.1 reshape_squeeze.8
  11.6 0.1 stack.27
  11.6 0.1 reshape_squeeze.9
  11.7 0.1 stack.29
  11.8 0.6 pad_maximum_fusion.2.ghost_out
  12.4 7.2 %shard_map.37 = (s32[8,8,128]{2,1,0:T(8,128)}, f32[2,2,128]{2,1,0:T(2,128)}) custom-call(s32[8,128]{1,0:T(8,128)} %broadcast_in_dim.12.mine, f32[2,2,128]{2,1,0:T(2,128)} %pad_maximum_fusion.2.ghost_out), custom_call_target="tpu_custom_call" | custom-call | tf_op jit(solution)/shard_map/pallas_call | solution.py:427
  19.6 1.0 %slice_reduce_fusion.1 = s32[8]{0:T(128)S(1)} fusion(s32[8,8,128]{2,1,0:T(8,128)} %get-tuple-element.7), kind=kLoop, calls=%fused_computation.7 | loop fusion | bytes 64 | tf_op jit(solution)/shard_map/slice | solution.py:436
  20.6 0.6 fusion.3
  21.9 0.6 pad_add_fusion.drift
  22.5 60.4 %shard_map.38 = f32[8,8,8,8,128]{4,3,2,1,0:T(8,128)} custom-call(s32[2]{0:T(128)} %pad_add_fusion.drift, f32[512]{0:T(512)} %bitcast.28, f32[2,6144,128]{2,1,0:T(8,128)} %bitcast.25, f32[6144,128]{1,0:T(8,128)} %bitcast.27), custom_call_target="tpu_custom_call" | custom-call | tf_op jit(solution)/shard_map/pallas_call | solution.py:448
  82.9 4.3 %copy.8 = f32[512,1,1024]{2,1,0:T(1,128)} copy(f32[512,1,1024]{2,1,0:T(1,128)} %bitcast.26) | data formatting | bytes 4194304
  (4 shorter events, 0.0 us)

commit v3 on v2

--- a/solution.py
+++ b/solution.py
@@ -17,58 +17,10 @@
 MESH = pl.DeviceIdType.MESH
 
 
-def gather_counts(n, mine, ghost_out, every, ghost_in, send_sem, recv_sem, ghost_send, ghost_recv):
-    me = lax.axis_index("curve")
-    barrier = pltpu.get_barrier_semaphore()
-    for off in range(1, n):
-        peer = lax.rem(me + off, n)
-        pl.semaphore_signal(barrier, inc=1, device_id={"curve": peer}, device_id_type=MESH)
-    pl.semaphore_wait(barrier, n - 1)
-    has_left, has_right = me > 0, me < n - 1
-    ghosts = []
-    for side, device in ((0, {"curve": me - 1}), (1, {"curve": me + 1})):
-        ghosts.append(
-            pltpu.make_async_remote_copy(
-                src_ref=ghost_out.at[side], dst_ref=ghost_in.at[1 - side],
-                send_sem=ghost_send.at[side], recv_sem=ghost_recv.at[side],
-                device_id=device, device_id_type=MESH,
-            )
-        )
-    for there, copy in zip((has_left, has_right), ghosts):
-        @pl.when(there)
-        def _():
-            copy.start()
-    copies = []
-    for off in range(1, n):
-        copies.append(
-            pltpu.make_async_remote_copy(
-                src_ref=mine,
-                dst_ref=every.at[me],
-                send_sem=send_sem.at[off],
-                recv_sem=recv_sem.at[off],
-                device_id={"curve": lax.rem(me + off, n)},
-                device_id_type=MESH,
-            )
-        )
-        copies[-1].start()
-    every[me] = mine[...]
-    for there, at in ((has_left, 0), (has_right, 1)):
-        @pl.when(jnp.logical_not(there))
-        def _():
-            ghost_in[at] = jnp.zeros(ghost_in.shape[1:], jnp.float32)
-    for copy in copies:
-        copy.wait()
-    for there, back, forth in ((has_left, 1, 0), (has_right, 0, 1)):
-        @pl.when(there)
-        def _():
-            ghosts[back].wait_recv()
-            ghosts[forth].wait_send()
-
-
 def exchange(
-    n, groups, cap_rows, drift, ghost, state, coef, out, raw0, raw1, raw2, wide0, wide1, source,
+    n, groups, cap_rows, counts, mine, state, coef, out, every, every_s, ends, met, ghost, raw0, raw1, raw2, wide0, wide1, source,
     inverse, out0, out1, out2, out3, in0, in1, in2, in3, face0, face1, near0, near1, inv, first_fix,
-    second_fix, result, edge_out, edge_in, load_sem, send_sem, recv_sem, face_send, face_recv, out_sem,
+    second_fix, result, edge_out, edge_in, count_send, count_recv, end_send, end_recv, local_sem, load_sem, send_sem, recv_sem, face_send, face_recv, out_sem,
 ):
     cells = SIDE * SIDE * SIDE
     own_rows = AVG // LANES
@@ -92,15 +44,76 @@
         @pl.when(there)
         def _():
             pl.semaphore_signal(barrier, inc=1, device_id=device, device_id_type=MESH)
-    pl.semaphore_wait(barrier, sum(there.astype(jnp.int32) for there, _ in sides))
-
-    drift_prev, drift_next = drift[0], drift[1]
+    for off in range(2, n - 1):
+        peer = lax.rem(rank + off, n)
+        pl.semaphore_signal(barrier, inc=1, device_id={"curve": peer}, device_id_type=MESH)
+    for there, peer in ((has_left, n - 1), (has_right, 0)):
+        @pl.when(jnp.logical_not(there))
+        def _():
+            pl.semaphore_signal(barrier, inc=1, device_id={"curve": peer}, device_id_type=MESH)
+    pl.semaphore_wait(barrier, n - 1 + has_low.astype(jnp.int32) + has_high.astype(jnp.int32))
+
+    tallies = []
+    for off in range(1, n):
+        tallies.append(
+            pltpu.make_async_remote_copy(
+                src_ref=mine, dst_ref=every.at[rank], send_sem=count_send.at[off],
+                recv_sem=count_recv.at[off], device_id={"curve": lax.rem(rank + off, n)},
+                device_id_type=MESH,
+            )
+        )
+        tallies[-1].start()
+    keep = pltpu.make_async_copy(mine, every.at[rank], local_sem.at[0])
+    keep.start()
+    lane = lax.broadcasted_iota(jnp.int32, (8, LANES), 1)
+    row = lax.broadcasted_iota(jnp.int32, (8, LANES), 0)
+    held = counts[0, 0]
+    last = jnp.clip(held - 1, 0, cap_rows * LANES - 1)
+    last_row = lax.shift_right_logical(last, 7)
+    last_turn = (LANES - (last & (LANES - 1))) & (LANES - 1)
+    for f in range(3):
+        loads[f].wait()
+    for side, at, turn, outer_x, near_x in ((0, 0, 0, 1, 0), (1, last_row, last_turn, SIDE - 2, SIDE - 1)):
+        packed = jnp.zeros((8, LANES), jnp.float32)
+        for p, (f, x) in enumerate(((0, outer_x), (0, near_x), (1, near_x), (2, near_x))):
+            for y in range(SIDE):
+                base = (x * (SIDE * SIDE) + y * SIDE) * cap_rows + PAD + at
+                value = raw[f][pl.ds(base, 8, stride=cap_rows), :]
+                if f == 2:
+                    value = 1.0 / (6.0 + value)
+                spot = p * SIDE + y
+                if side:
+                    value = pltpu.roll(value, (turn + spot) & (LANES - 1), 1)
+                elif spot:
+                    value = pltpu.roll(value, spot, 1)
+                packed = jnp.where(lane == spot, value, packed)
+        ends[side] = packed
+
+    def greeted(side):
+        return pltpu.make_async_remote_copy(
+            src_ref=ends.at[side], dst_ref=met.at[1 - side], send_sem=end_send.at[side],
+            recv_sem=end_recv.at[side], device_id=sides[side][1], device_id_type=MESH,
+        )
+
+    for side in range(2):
+        @pl.when(sides[side][0])
+        def _():
+            greeted(side).start()
+    keep.wait()
+    for copy in tallies:
+        copy.wait()
+    keep = pltpu.make_async_copy(every, every_s, local_sem.at[1])
+    keep.start()
+    keep.wait()
+    before = 0
+    for r in range(n):
+        before = before + jnp.where(r < rank, every_s[r, 0, 0], 0)
+    drift_prev = jnp.clip(before - rank * AVG, -HALF, HALF)
+    drift_next = drift_prev + held - AVG
     shift = 8 * LANES - LEAD * LANES - drift_prev
     first = lax.shift_right_logical(shift, 7) - 8 + PAD
     part = shift & (LANES - 1)
     turn = (LANES - part) & (LANES - 1)
-    lane = lax.broadcasted_iota(jnp.int32, (8, LANES), 1)
-    row = lax.broadcasted_iota(jnp.int32, (8, LANES), 0)
     stay = lane >= part
     low_rows, high_rows = pl.ds(0, 8), pl.ds(8, 8)
     own = pl.ds(LEAD, own_rows)
@@ -155,7 +168,6 @@
                     put[1, p, x, z] = get(x, y, z, pl.ds(8 + to_right, half_rows))
 
     outer, near_outer = (0, SIDE - 1), (0, 1, SIDE - 2, SIDE - 1)
-    loads[0].wait()
 
     def step(x, y):
         for z in range(SIDE):
@@ -164,7 +176,6 @@
     each(step)
     pack(out0, lambda x, y, z, rows: wide0[x + 1, y + 1, z, rows, :], outer)
     send(0)
-    loads[2].wait()
 
     def step(x, y):
         for z in range(SIDE):
@@ -173,7 +184,6 @@
     each(step)
     pack(out1, lambda x, y, z, rows: inverse[x, y, z, rows, :], near_outer)
     send(1)
-    loads[1].wait()
 
     def step(x, y):
         for z in range(SIDE):
@@ -181,6 +191,14 @@
             source[x, y, z, high_rows, :] = aligned(1, x, y, z, 1)
     each(step)
 
+    for side in range(2):
+        @pl.when(sides[side][0])
+        def _():
+            greeted(1 - side).wait_recv()
+            greeted(side).wait_send()
+    keep_ends = pltpu.make_async_copy(met, ghost, local_sem.at[2])
+    keep_ends.start()
+    keep_ends.wait()
     block = row * LANES + lane - LEAD * LANES
     for side, at, planes in (
         (0, drift_prev - 1, ((wide0, 1, SIDE - 1), (wide0, 1, SIDE), (source, 0, SIDE - 1), (inverse, 0, SIDE - 1))),
@@ -191,7 +209,7 @@
             @pl.loop(0, SIDE)
             def _(y):
                 for z in range(SIDE):
-                    value = ghost[side * 4 * SIDE * SIDE + p * SIDE * SIDE + y * SIDE + z]
+                    value = jnp.where(sides[side][0], ghost[side, z, p * SIDE + y], 0.0)
                     for half, rows in enumerate((low_rows, high_rows)):
                         old = ref[x, y + off, z, rows, :]
                         ref[x, y + off, z, rows, :] = jnp.where(here[half], value, old)
@@ -408,34 +426,11 @@
 
 def local(state, coef, counts):
     n, groups = lax.axis_size("curve"), lax.axis_size("grp")
-    rank = lax.axis_index("curve")
     cells, cap = state.shape[1], state.shape[3]
     cap_rows, own_rows, half_rows = cap // LANES, AVG // LANES, HALF // LANES
-    plane = SIDE * SIDE
-    held = counts[0, 0]
     f32 = jnp.float32
-
-    def end_block(at, outer, near):
-        cell = lax.dynamic_slice_in_dim(state, at, 1, 3)[:, :, 0, 0].reshape(2, SIDE, plane)
-        scale = lax.dynamic_slice_in_dim(coef, at, 1, 2)[:, 0, 0].reshape(SIDE, plane)
-        return jnp.stack([cell[0, outer], cell[0, near], cell[1, near], 1.0 / (6.0 + scale[near])])
-
-    ends = jnp.stack([end_block(0, 1, 0), end_block(held - 1, SIDE - 2, SIDE - 1)])
-    ends = ends.reshape(2, 4 * plane // LANES, LANES)
-    mine = jnp.broadcast_to(counts, (8, LANES))
+    mine = jnp.broadcast_to(counts, (1, LANES))
     vmem, hbm, smem = (pl.BlockSpec(memory_space=m) for m in (pltpu.VMEM, pl.ANY, pltpu.SMEM))
-    every, ghost = pl.pallas_call(
-        functools.partial(gather_counts, n),
-        out_shape=(jax.ShapeDtypeStruct((n, 8, LANES), jnp.int32), jax.ShapeDtypeStruct(ends.shape, f32)),
-        in_specs=[vmem, vmem],
-        out_specs=(vmem, vmem),
-        scratch_shapes=[pltpu.SemaphoreType.DMA((k,)) for k in (n, n, 2, 2)],
-        compiler_params=pltpu.CompilerParams(collective_id=0, has_side_effects=True),
-    )(mine, ends)
-    order = jnp.arange(n, dtype=jnp.int32)
-    before = jnp.sum(jnp.where(order < rank, every[:, 0, 0], 0))
-    drift_prev = before - rank * AVG
-    drift = jnp.stack([drift_prev, drift_prev + held - AVG])
     side = (SIDE, SIDE)
     packed = [(2, 2) + side, (2, 4) + side, (2, 2) + side, (2, SIDE) + side]
     packed = [shape + (half_rows, LANES) for shape in packed]
@@ -448,16 +443,23 @@
     out = pl.pallas_call(
         functools.partial(exchange, n, groups, cap_rows),
         out_shape=jax.ShapeDtypeStruct((SIDE, SIDE, SIDE, own_rows, LANES), f32),
-        in_specs=[smem, smem, hbm, hbm],
+        in_specs=[smem, vmem, hbm, hbm],
         out_specs=hbm,
-        scratch_shapes=[pltpu.VMEM(shape, f32) for shape in shapes]
-        + [pltpu.SemaphoreType.DMA((k,)) for k in (3, 8, 8, 6, 6)]
+        scratch_shapes=[
+            pltpu.VMEM((n, 1, LANES), jnp.int32),
+            pltpu.SMEM((n, 1, LANES), jnp.int32),
+            pltpu.VMEM((2, 8, LANES), f32),
+            pltpu.VMEM((2, 8, LANES), f32),
+            pltpu.SMEM((2, 8, LANES), f32),
+        ]
+        + [pltpu.VMEM(shape, f32) for shape in shapes]
+        + [pltpu.SemaphoreType.DMA((k,)) for k in (n, n, 2, 2, 3, 3, 8, 8, 6, 6)]
         + [pltpu.SemaphoreType.DMA],
         compiler_params=pltpu.CompilerParams(
-            collective_id=1, has_side_effects=True, vmem_limit_bytes=56 * 1024 * 1024
+            collective_id=0, has_side_effects=True, vmem_limit_bytes=48 * 1024 * 1024
         ),
     )(
-        drift, ghost.reshape(-1), state.reshape(2, cells * cap_rows, LANES),
+        counts, mine, state.reshape(2, cells * cap_rows, LANES),
         coef.reshape(cells * cap_rows, LANES),
     )
     return out.reshape(cells, 1, AVG)

time: 87.6 us -> 66.4 us (0.76)
  local copies, waits for them, and re-layouts: 14.6 us -> 3.21 us
  Pallas kernels: 67.6 us -> 62.3 us
  other arithmetic: 3.72 us -> 0 us
    dynamic_slice x1 -> x0, local copies, waits for them, and re-layouts: 8.34 us -> none  [end_block(): lax.dynamic_slice_in_dim(state, at, 1, 3)[:, :, 0, 0]]
    pallas_call x1 -> x0, Pallas kernels: 7.22 us -> none  [local(): pl.pallas_call(functools.partial(gather_counts, n), out_shape=(jax.ShapeD...]
    pallas_call x1, Pallas kernels: 60.4 us -> 62.3 us  [local(): pl.pallas_call(functools.partial(exchange, n, groups, cap_rows), out_shap...]
    div x1 -> x0, other arithmetic: 1.86 us -> none  [end_block(): 1.0 / (6.0 + scale[near])]
    another operation x4 -> x0, other arithmetic: 1.21 us -> none  [the longest x1 0.62 us: local(): drift = jnp.stack([drift_prev, drift_prev + held - AVG])]
    unnamed x1 -> x3, local copies, waits for them, and re-layouts: 4.35 us -> 3.21 us
    slice x1 -> x0, local copies, waits for them, and re-layouts: 0.99 us -> none  [local(): before = jnp.sum(jnp.where(order < rank, every[:, 0, 0], 0))]
where the time goes in v3:
time: 66.4 us; the launch traced here: 66.2 us
  Pallas kernels  62.3 us (94%)
  local copies, waits for them, and re-layouts  3.21 us (5%)
  between operations  0.68 us (1%)
    pallas_call x1, Pallas kernels, local(): pl.pallas_call(functools.partial(exchange, n, groups, cap_rows), out_shap...  62.3 us
    unnamed x3, local copies, waits for them, and re-layouts  3.21 us

profile of v3, /device:TPU:9, one launch (start us, length us, event | category | flops | bytes accessed | tf_op | source)
XLA Modules:
  0.0 66.2 jit_solution(6818404285082681273)
XLA Ops:
  0.7 0.0 copy-start
  0.7 1.9 %copy-done = f32[512,1,1536]{2,1,0:T(1,128)S(1)} copy-done((f32[512,1,1536]{2,1,0:T(1,128)S(1)}, f32[512,1,1536]{2,1,0:T(1,128)}, u32[]{:S(2)}) %copy-start) | copy-done | bytes 3145752
  2.6 62.3 %shard_map.37 = f32[8,8,8,8,128]{4,3,2,1,0:T(8,128)S(1)} custom-call(s32[1,1]{1,0:T(1,128)} %copy.6.counts, s32[1,128]{1,0:T(1,128)S(1)} %broadcast_in_dim.8.mine, f32[2,6144,128]{2,1,0:T(8,128)} %bitcast.7, f32[6144,128]{1,0:T(8,128)S(1)} %bitcast.6), custom_call_target="tpu_custom_call" | custom-call | tf_op jit(solution)/shard_map/pallas_call | solution.py:443
  64.9 1.3 %copy.7 = f32[512,1,1024]{2,1,0:T(1,128)} copy(f32[512,1,1024]{2,1,0:T(1,128)S(1)} %bitcast.5) | data formatting | bytes 4194304
  (1 shorter events, 0.0 us)
Async XLA Ops:
  0.7 1.9 %copy-start = (f32[512,1,1536]{2,1,0:T(1,128)S(1)}, f32[512,1,1536]{2,1,0:T(1,128)}, u32[]{:S(2)}) copy-start(f32[512,1,1536]{2,1,0:T(1,128)} %param.4) | copy-start | bytes 9437188
